TPU v7x, 32 devices: a whole 2x2x4 slice. The times are simulated.
32 devices in a mesh: beam: 2 (over x), freq: 8 (over z, y), sub: 2 (over core).
Axes of the slice: x: 2, y: 2, z: 4, core: 2. Of those that a mesh axis runs over, the one named last changes fastest.
Arguments:
- spectrum: bfloat16 [64, 2097152], P('sub', ('beam', 'freq')), parts along dimension 1
- hit_mask: int32 [64, 16384], P('sub', ('beam', 'freq')), parts along dimension 1, may hold values from 0 to 1, as said below
- owner_map: int32 [2048], P(('beam', 'freq')), parts along dimension 0, may hold values from 0 to 1023, as said below
- median_bin: int32 [2048], P(('beam', 'freq')), parts along dimension 0, may hold values from 32 to 559
- mad_bin: int32 [2048], P(('beam', 'freq')), parts along dimension 0, may hold values from 4 to 15
Outputs:
- hit_snr: bfloat16 [8, 2, 2048, 128], P('freq', 'sub', 'beam'), parts along dimension 2
- hit_keys: int32 [8, 2, 2048], P('freq', 'sub', 'beam'), parts along dimension 2
- hit_excess: float32 [8, 2, 2048], P('freq', 'sub', 'beam'), parts along dimension 2
There are 2 independent parts, one for each index of `beam`. A program takes and returns all parts, laid end to end along the dimension named above; each array names one. Nothing has to cross between parts.
Inputs may be any that keep to these rules, and one draw needn't show every extreme that they name: `hit_mask`: for each index of freq, each half of the drift rates and each owner, at most 128 hit blocks go from the first to the last; in every draw some owner gets exactly 128 from every index of freq and half. `owner_map`: A permutation of the slots 0 to 1023; the 128 coarse channels of one index of freq go 16 to each owner, and the slot of index f's coarse channel at each owner is f.
All inputs are finite; a program needn't handle non-finite values.
Results may differ from a plain program's by a relative error of at most 0.007.
Values may be sent and summed in bfloat16 or wider, within the bound.
A program may use at most 64 MiB of HBM per device.

v0:
```python
import jax
import jax.numpy as jnp
from jax import lax
from jax.sharding import PartitionSpec as P

COARSE_WIDTH = 1024
BLOCK = 128
CAP = 128


BIN_STEP = 0.0625
MAD_WIDTH = 5.0
MAD_SCALE = 1.4826
THRESH = 3.0


def pick_from(selector, table):
    return jnp.sum(selector * table[None, :], axis=1)


def per_device(spectrum, hit_mask, owner_map, median_bin, mad_bin):
    drift_dev = spectrum.shape[0]
    coarse_dev = owner_map.shape[0]
    per_coarse = COARSE_WIDTH // BLOCK
    freq_count = lax.axis_size("freq")
    drift_total = drift_dev * lax.axis_size("sub")
    half_index = lax.axis_index("sub")
    slots_total = freq_count * CAP
    power = spectrum.astype(jnp.float32).reshape(drift_dev, coarse_dev, COARSE_WIDTH)
    center = BIN_STEP * median_bin.astype(jnp.float32)
    spread = MAD_WIDTH * BIN_STEP * mad_bin.astype(jnp.float32)
    inside = (power >= (center - spread)[None, :, None]) & (
        power <= (center + spread)[None, :, None]
    )
    kept = jnp.where(inside, power - center[None, :, None], 0.0)
    window_count = jnp.sum(inside.astype(jnp.float32), axis=(0, 2))
    first = jnp.sum(kept, axis=(0, 2))
    second = jnp.sum(kept * kept, axis=(0, 2))
    window_count, first, second = lax.psum((window_count, first, second), "sub")
    floor_count = jnp.maximum(window_count, 1.0)
    mean_level = center + first / floor_count
    mad_sigma = MAD_SCALE * BIN_STEP * mad_bin.astype(jnp.float32)
    sigma = jnp.sqrt(0.5 * second / floor_count + 0.5 * mad_sigma * mad_sigma)
    marks = hit_mask.reshape(drift_dev, coarse_dev, per_coarse)
    row_count = jnp.sum(marks, axis=2)
    coarse_count = jnp.sum(row_count, axis=0)
    row_start = jnp.cumsum(row_count, axis=0) - row_count
    dest = owner_map // coarse_dev
    slot_local = owner_map % coarse_dev
    ahead = ((dest[None, :] == dest[:, None]) & (slot_local[None, :] < slot_local[:, None])).astype(
        jnp.int32
    )
    offset = jnp.sum(ahead * coarse_count[None, :], axis=1)
    positions = jnp.arange(slots_total, dtype=jnp.int32)
    target_dest = positions // CAP
    within = positions % CAP
    select = (
        (dest[None, :] == target_dest[:, None])
        & (offset[None, :] <= within[:, None])
        & (within[:, None] < (offset + coarse_count)[None, :])
    )
    filled = jnp.any(select, axis=1)
    pick = select.astype(jnp.int32)
    coarse_ids = jnp.arange(coarse_dev, dtype=jnp.int32)
    chosen_coarse = pick_from(pick, coarse_ids)
    chosen_slot = pick_from(pick, slot_local)
    remain = within - pick_from(pick, offset)
    pick_float = pick.astype(jnp.float32)
    starts_at = jnp.dot(
        pick_float, row_start.T.astype(jnp.float32), precision=lax.Precision.HIGHEST
    ).astype(jnp.int32)
    counts_at = jnp.dot(
        pick_float, row_count.T.astype(jnp.float32), precision=lax.Precision.HIGHEST
    ).astype(jnp.int32)
    row_pick = ((starts_at <= remain[:, None]) & (remain[:, None] < starts_at + counts_at)).astype(
        jnp.int32
    )
    chosen_drift = pick_from(row_pick, jnp.arange(drift_dev, dtype=jnp.int32))
    inner = remain - jnp.sum(row_pick * starts_at, axis=1)
    bit_rows = marks.reshape(-1, per_coarse)[chosen_drift * coarse_dev + chosen_coarse]
    bit_before = jnp.cumsum(bit_rows, axis=1) - bit_rows
    bit_pick = ((bit_rows > 0) & (bit_before == inner[:, None])).astype(jnp.int32)
    chosen_block = pick_from(bit_pick, jnp.arange(per_coarse, dtype=jnp.int32))
    source_row = jnp.where(
        filled, (chosen_drift * coarse_dev + chosen_coarse) * per_coarse + chosen_block, 0
    )
    slot_keys = jnp.where(
        filled,
        (chosen_slot * drift_total + half_index * drift_dev + chosen_drift) * per_coarse
        + chosen_block,
        -1,
    )
    blocks = spectrum.reshape(-1, BLOCK)[source_row]
    level = jnp.sum(pick_float * mean_level[None, :], axis=1)
    scale = jnp.where(filled, jnp.sum(pick_float * sigma[None, :], axis=1), 1.0)
    normal = (blocks.astype(jnp.float32) - level[:, None]) / scale[:, None]
    payload = jnp.where(filled[:, None], normal, 0.0).astype(jnp.bfloat16)
    arrived = lax.all_to_all(
        payload.reshape(freq_count, CAP, BLOCK), "freq", split_axis=0, concat_axis=0, tiled=True
    )
    keys = lax.all_to_all(
        slot_keys.reshape(freq_count, CAP), "freq", split_axis=0, concat_axis=0, tiled=True
    )
    excess = jnp.sum(jnp.maximum(arrived.astype(jnp.float32) - THRESH, 0.0), axis=-1)
    hit_rows, arrived_keys, excess = (arrived, keys, excess)
    got = jnp.sum((arrived_keys >= 0).astype(jnp.int32), axis=1)
    ends = jnp.cumsum(got)
    begins = ends - got
    source_of = jnp.sum((ends[None, :] <= positions[:, None]).astype(jnp.int32), axis=1)
    live = source_of < freq_count
    source_clip = jnp.minimum(source_of, freq_count - 1)
    source_hot = (jnp.arange(freq_count, dtype=jnp.int32)[None, :] == source_clip[:, None]).astype(
        jnp.int32
    )
    begin_of = jnp.sum(source_hot * begins[None, :], axis=1)
    take = jnp.where(live, source_clip * CAP + positions - begin_of, 0)
    hit_snr = jnp.where(
        live[:, None], hit_rows.reshape(-1, BLOCK)[take], jnp.zeros((1, BLOCK), jnp.bfloat16)
    )
    hit_keys = jnp.where(live, arrived_keys.reshape(-1)[take], -1).astype(jnp.int32)
    hit_excess = jnp.where(live, excess.reshape(-1)[take], 0.0)
    return (
        hit_snr.reshape(1, 1, slots_total, BLOCK),
        hit_keys.reshape(1, 1, slots_total),
        hit_excess.reshape(1, 1, slots_total),
    )


def solution(mesh):
    placed = (
        P("sub", ("beam", "freq")),
        P("sub", ("beam", "freq")),
        P(("beam", "freq")),
        P(("beam", "freq")),
        P(("beam", "freq")),
    )
    return jax.shard_map(
        per_device,
        mesh=mesh,
        in_specs=placed,
        out_specs=(
            P("freq", "sub", "beam", None),
            P("freq", "sub", "beam"),
            P("freq", "sub", "beam"),
        ),
        check_vma=False,
    )
```

profile of v0, /device:TPU:0, one launch (start us, length us, event | category | flops | bytes accessed | tf_op | source)
XLA Modules:
  0.0 81.4 jit_solution(6985785107523849419)
XLA Ops:
  0.6 1.1 %copy.19 = s32[32,1024]{0,1:T(8,128)S(1)} copy(s32[32,1024]{1,0:T(8,128)} %param.6) | data formatting | bytes 262144 | tf_op args[1]
  1.8 2.0 %reshape_reshape.3 = s32[4096,8]{1,0:T(8,128)S(1)} reshape(s32[32,1024]{1,0:T(8,128)} %param.6) | data formatting | bytes 262144 | tf_op jit(solution)/shard_map/reshape;reshape | solution.py:80
  3.8 0.7 and_select_fusion.1
  4.5 0.9 %reduce_sum.198 = s32[1024]{0:T(1024)S(1)} reduce(s32[32,1024]{1,0:T(8,128)} %param.6, s32[]{:T(128)} %constant.89.clone.1), dimensions={0}, to_apply=%region_0.1 | reduce | flops 31744 | bytes 135172 | tf_op jit(solution)/shard_map/reduce_sum | solution.py:46
  5.8 0.7 fusion.28
  7.4 10.7 %fusion.2 = (f32[131072]{0:T(1024)}, f32[131072]{0:T(1024)}, f32[131072]{0:T(1024)S(1)}) fusion(bf16[32,131072]{1,0:T(8,128)(2,1)} %param.5, f32[131072]{0:T(1024)S(1)} %bitcast.43, f32[131072]{0:T(1024)S(1)} %bitcast.44, f32[131072]{0:T(1024)S(1)} %bitcast.42), kind=kLoop, calls=%fused_computation.10 | loop fusion | flops 45744128 | bytes 11534336 | tf_op jit(solution)/shard_map/reduce_sum | solution.py:37
  18.1 1.1 %reduce_sum.214 = f32[128,1024]{1,0:T(8,128)S(1)} reshape(f32[131072]{0:T(1024)} %get-tuple-element.3) | data formatting | bytes 1048576 | tf_op jit(solution)/shard_map/reduce_sum | solution.py:37
  19.2 1.9 %reduce_sum.221 = f32[128,1024]{1,0:T(8,128)} reshape(f32[131072]{0:T(1024)} %get-tuple-element.4) | data formatting | bytes 1048576 | tf_op jit(solution)/shard_map/reduce_sum | solution.py:38
  21.3 1.2 %reduce_sum.222 = f32[128]{0:T(128)S(1)} reduce(f32[128,1024]{1,0:T(8,128)} %reduce_sum.221, f32[]{:T(128)} %constant.103.clone.1), dimensions={1}, to_apply=%region_24.25 | reduce | flops 130944 | bytes 524804 | tf_op jit(solution)/shard_map/reduce_sum | solution.py:38
  22.6 2.6 %all-reduce = (f32[128]{0:T(128)S(1)}, f32[128]{0:T(128)S(1)}, f32[128]{0:T(128)S(1)}) all-reduce(f32[128]{0:T(128)S(1)} %reduce_sum.215, f32[128]{0:T(128)S(1)} %reduce_sum.218, f32[128]{0:T(128)S(1)} %reduce_sum.222), channel_id=1, replica_groups=mesh['beam'=2,'freq'=8,'sub'=2] {'sub'}, use_global_device_ids=true, to_apply=%region_18.19 | all-reduce | flops 384 | bytes 3072 | tf_op jit(solution)/shard_map/psum | solution.py:39
  25.3 1.0 %multiply_reduce_fusion.1 = (f32[1024]{0:T(1024)S(1)}, f32[1024]{0:T(1024)S(1)}, pred[1024,128]{1,0:T(32,128)(4,1)S(1)}) fusion(f32[128]{0:T(128)S(1)} %get-tuple-element.24, f32[128]{0:T(128)S(1)} %get-tuple-element.23, s32[128]{0:T(128)S(1)} %add.174, s32[1024]{0:T(1024)S(1)} %get-tuple-element.28, s32[128]{0:T(128)S(1)} %select_reduce_fusion.7, ...), kind=kLoop, calls=%fused_computation.28 | loop fusion | flops 1439744 | bytes 150016 | tf_op jit(solution)/shard_map/reduce_sum | solution.py:94
  26.3 0.5 select_reduce_fusion.4
  26.8 0.7 convolution_convert_fusion.1
  27.5 0.7 select_reduce_fusion.5
  28.2 2.8 %gather_fusion = s32[1024,8]{1,0:T(8,128)S(1)} fusion(s32[4096,8]{1,0:T(8,128)S(1)} %reshape_reshape.3, s32[1024]{0:T(1024)S(1)} %broadcast_clamp_fusion.2), kind=kCustom, calls=%fused_computation | custom fusion | bytes 69632 | tf_op jit(solution)/shard_map/gather | solution.py:80
  31.0 0.3 reduce_window_sum.30
  31.4 0.2 reduce_or.13
  31.6 0.4 select_reduce_fusion.1
  32.0 0.6 add_select_fusion.1
  32.6 7.2 %all-to-all-start = ((s32[8,1,128]{2,1,0:T(1,128)}), s32[8,1,128]{2,1,0:T(1,128)S(1)}, u32[]{:S(2)}, u32[]{:S(2)}) async-start(s32[8,1,128]{2,1,0:T(1,128)} %bitcast.3), calls=%async_computation | async-start | bytes 8192 | tf_op jit(solution)/shard_map/all_to_all | solution.py:101
  39.8 8.9 %reshape.376 = bf16[32768,128]{1,0:T(8,128)(2,1)} reshape(bf16[32,131072]{1,0:T(8,128)(2,1)} %param.5) | data formatting | bytes 16777216 | tf_op jit(solution)/shard_map/reshape | solution.py:93
  48.7 7.3 %gather_fusion.1 = bf16[1024,128]{1,0:T(8,128)(2,1)S(1)} fusion(bf16[32768,128]{1,0:T(8,128)(2,1)} %reshape.376, s32[1024]{0:T(1024)S(1)} %broadcast_clamp_fusion.1), kind=kCustom, calls=%fused_computation.1 | custom fusion | bytes 528384 | tf_op jit(solution)/shard_map/gather | solution.py:93
  56.1 1.2 %fusion.10 = bf16[8,128,128]{2,1,0:T(8,128)(2,1)} fusion(bf16[8,128,128]{2,1,0:T(8,128)(2,1)S(1)} %bitcast.46, f32[8,128]{1,0:T(8,128)S(1)} %bitcast_select_fusion.1, f32[8,128]{1,0:T(8,128)S(1)} %bitcast.51, pred[8,128]{1,0:T(8,128)(4,1)S(1)} %bitcast.50), kind=kLoop, calls=%fused_computation.22 | loop fusion | flops 655360 | bytes 533504 | tf_op jit(solution)/shard_map/convert_element_type | solution.py:97
  57.3 6.0 %all-to-all-start.1 = ((bf16[8,128,128]{2,1,0:T(8,128)(2,1)}), bf16[8,128,128]{2,1,0:T(8,128)(2,1)S(1)}, u32[]{:S(2)}, u32[]{:S(2)}) async-start(bf16[8,128,128]{2,1,0:T(8,128)(2,1)} %fusion.10), calls=%async_computation.1 | async-start | bytes 524288 | tf_op jit(solution)/shard_map/all_to_all | solution.py:98
  63.7 0.4 select_reduce_fusion
  64.1 4.5 %gather_fusion.3 = s32[1024]{0:T(1024)S(1)} fusion(s32[1024]{0:T(1024)S(1)} %bitcast.39, s32[1024]{0:T(1024)S(1)} %broadcast_clamp_fusion), kind=kCustom, calls=%fused_computation.3 | custom fusion | bytes 12288 | tf_op jit(solution)/shard_map/gather | solution.py:120
  68.6 0.6 broadcast_select_fusion.1
  69.2 2.7 %all-to-all-done.1 = bf16[8,128,128]{2,1,0:T(8,128)(2,1)S(1)} async-done(((bf16[8,128,128]{2,1,0:T(8,128)(2,1)}), bf16[8,128,128]{2,1,0:T(8,128)(2,1)S(1)}, u32[]{:S(2)}, u32[]{:S(2)}) %all-to-all-start.1) | async-done | bytes 262176 | tf_op jit(solution)/shard_map/all_to_all | solution.py:98
  72.2 4.5 %gather_fusion.4 = f32[1024]{0:T(1024)S(1)} fusion(f32[1024]{0:T(1024)S(1)} %bitcast.40, s32[1024]{0:T(1024)S(1)} %broadcast_clamp_fusion), kind=kCustom, calls=%fused_computation.4 | custom fusion | bytes 12288 | tf_op jit(solution)/shard_map/gather | solution.py:121
  76.7 3.2 %gather_fusion.2 = bf16[1024,128]{1,0:T(8,128)(2,1)S(1)} fusion(bf16[1024,128]{1,0:T(8,128)(2,1)S(1)} %bitcast.41, s32[1024]{0:T(1024)S(1)} %broadcast_clamp_fusion), kind=kCustom, calls=%fused_computation.2 | custom fusion | bytes 528384 | tf_op jit(solution)/shard_map/gather | solution.py:118
  79.9 0.6 broadcast_select_fusion
  80.5 0.9 %bitcast_select_fusion = bf16[1,1,1024,128]{3,2,1,0:T(8,128)(2,1)} fusion(bf16[1024,128]{1,0:T(8,128)(2,1)S(1)} %gather_fusion.2, pred[1024]{0:T(1024)(128)(4,1)S(1)} %broadcast_compare_fusion), kind=kLoop, calls=%fused_computation.40 | loop fusion | flops 131072 | bytes 525312 | tf_op jit(solution)/shard_map/jit(_where)/select_n | solution.py:117
  (39 shorter events, 2.2 us)
Async XLA Ops:
  7.3 17.9 %copy-start = (s32[128]{0:T(128)S(1)}, s32[128]{0:T(128)}, u32[]{:S(2)}) copy-start(s32[128]{0:T(128)} %param.9) | copy-start | bytes 1540
  7.3 17.9 %copy-start.1 = (s32[128]{0:T(128)S(1)}, s32[128]{0:T(128)}, u32[]{:S(2)}) copy-start(s32[128]{0:T(128)} %param.8) | copy-start | bytes 1540
  32.6 24.6 %all-to-all-start = ((s32[8,1,128]{2,1,0:T(1,128)}), s32[8,1,128]{2,1,0:T(1,128)S(1)}, u32[]{:S(2)}, u32[]{:S(2)}) async-start(s32[8,1,128]{2,1,0:T(1,128)} %bitcast.3), calls=%async_computation | async-start | bytes 8192 | tf_op jit(solution)/shard_map/all_to_all | solution.py:101
  57.3 14.7 %all-to-all-start.1 = ((bf16[8,128,128]{2,1,0:T(8,128)(2,1)}), bf16[8,128,128]{2,1,0:T(8,128)(2,1)S(1)}, u32[]{:S(2)}, u32[]{:S(2)}) async-start(bf16[8,128,128]{2,1,0:T(8,128)(2,1)} %fusion.10), calls=%async_computation.1 | async-start | bytes 524288 | tf_op jit(solution)/shard_map/all_to_all | solution.py:98
where the time goes:
time: 82 us; the launch traced here: 81.4 us
  local copies, waits for them, and re-layouts  38.3 us (47%)
  other arithmetic  22.3 us (27%)
  starting transfers between devices  13.1 us (16%)
  waiting for transfers between devices  2.74 us (3%)
  blocking collectives  2.63 us (3%)
  matrix products  1.37 us (2%)
  between operations  0.95 us (1%)
    reduce_sum x2, other arithmetic, per_device(): first = jnp.sum(kept, axis=(0, 2))  10.8 us
    reshape x1, local copies, waits for them, and re-layouts, per_device(): blocks = spectrum.reshape(-1, BLOCK)[source_row]  8.9 us
    gather x1, local copies, waits for them, and re-layouts, per_device(): blocks = spectrum.reshape(-1, BLOCK)[source_row]  7.34 us
    all_to_all x1, starting transfers between devices, per_device(): lax.all_to_all(slot_keys.reshape(freq_count, CAP), 'freq', split_axis=0,...  7.16 us
    all_to_all x1, starting transfers between devices, per_device(): lax.all_to_all(payload.reshape(freq_count, CAP, BLOCK), 'freq', split_axi...  5.99 us
    gather x1, local copies, waits for them, and re-layouts, per_device(): arrived_keys.reshape(-1)[take]  4.53 us
    gather x1, local copies, waits for them, and re-layouts, per_device(): hit_excess = jnp.where(live, excess.reshape(-1)[take], 0.0)  4.53 us
    gather x1, local copies, waits for them, and re-layouts, per_device(): hit_rows.reshape(-1, BLOCK)[take]  3.21 us
  transfers between devices with their start and end apart: 2, of which 1 were waited for; matrix products, arithmetic and copies ran while one was open for 29% of the time, Pallas kernels for 0%

commit v1 on v0

v1 whole, which is shorter than its diff:
```python
import functools

import jax
import jax.numpy as jnp
from jax import lax
from jax.experimental import pallas as pl
from jax.experimental.pallas import tpu as pltpu
from jax.sharding import PartitionSpec as P

COARSE_WIDTH = 1024
BLOCK = 128
CAP = 128
PER = COARSE_WIDTH // BLOCK

BIN_STEP = 0.0625
MAD_WIDTH = 5.0
MAD_SCALE = 1.4826
THRESH = 3.0

F32 = jnp.float32
BF16 = jnp.bfloat16
MESH = pl.DeviceIdType.MESH
NT = (((1,), (1,)), ((), ()))


def iota(shape, dim):
    return lax.broadcasted_iota(jnp.int32, shape, dim)


def one(mask, dtype=BF16):
    return jnp.where(mask, jnp.ones((), dtype), jnp.zeros((), dtype))


def positions(om_ref, mask_ref, turned, place):
    drifts = mask_ref.shape[0]
    coarse = place.shape[0]
    keys = PER * drifts
    turned[...] = mask_ref[...].astype(F32).T
    marks = jnp.concatenate([turned[pl.ds(b, coarse, stride=PER), :] for b in range(PER)], axis=1)
    rank_a = iota((keys, keys), 0)
    rank_b = iota((keys, keys), 1)
    rank_a = (rank_a % drifts) * PER + rank_a // drifts
    rank_b = (rank_b % drifts) * PER + rank_b // drifts
    before = jnp.dot(marks.astype(BF16), one(rank_a < rank_b), preferred_element_type=F32)
    count = jnp.sum(marks, axis=1, keepdims=True)
    wide = jnp.broadcast_to(om_ref[...], (coarse, coarse))
    eye = iota((coarse, coarse), 0) == iota((coarse, coarse), 1)
    tall = jnp.sum(jnp.where(eye, wide, 0), axis=1, keepdims=True)
    ahead = (wide // coarse == tall // coarse) & (wide < tall)
    offset = jnp.dot(
        one(ahead),
        jnp.broadcast_to(count, (coarse, keys)).astype(BF16),
        preferred_element_type=F32,
    )
    place[...] = jnp.where(marks > 0, offset + before, -1.0)


def local_kernel(
    om_s, med_s, mad_s, om_ref, mask_ref, spec_ref, rows_ref, tags_ref, mom_ref,
    turned, place, held, tagged, sums,
):
    step = pl.program_id(0)
    drifts = spec_ref.shape[0]
    coarse = place.shape[0]
    keys = PER * drifts
    chunk = spec_ref.shape[1] // COARSE_WIDTH

    @pl.when(step == 0)
    def _():
        positions(om_ref, mask_ref, turned, place)
        held[...] = jnp.zeros_like(held)
        tagged[...] = jnp.zeros_like(tagged)

    spot = iota((CAP, keys), 0).astype(F32).astype(BF16)
    lane = iota((8, keys), 1)
    row = iota((8, keys), 0)
    order = ((lane % drifts) * PER + lane // drifts).astype(F32)
    for k in range(chunk):
        c = step * chunk + k
        center = BIN_STEP * med_s[c].astype(F32)
        spread = MAD_WIDTH * BIN_STEP * mad_s[c].astype(F32)
        low, high = center - spread, center + spread
        total = [jnp.zeros((8, BLOCK), F32) for _ in range(3)]
        tiles = []
        for b in range(PER):
            tile = spec_ref[:, k * COARSE_WIDTH + b * BLOCK : k * COARSE_WIDTH + (b + 1) * BLOCK]
            tiles.append(tile)
            x = tile.astype(F32)
            inside = (x >= low) & (x <= high)
            kept = jnp.where(inside, x - center, 0.0)
            for i, v in enumerate((one(inside, F32), kept, kept * kept)):
                for r in range(0, drifts, 8):
                    total[i] = total[i] + v[r : r + 8]
        for i in range(3):
            sums[i, pl.ds(c, 1), :] = jnp.sum(total[i], axis=0, keepdims=True)
        line = jnp.broadcast_to(place[pl.ds(c, 1), :], (16, keys)).astype(BF16)
        pick = one(jnp.concatenate([line] * (CAP // 16), axis=0) == spot)
        dest = om_s[c] // coarse
        slot = (om_s[c] % coarse).astype(F32)
        held[dest] += jnp.dot(pick, jnp.concatenate(tiles, axis=0), preferred_element_type=F32)
        tag = jnp.where(
            row == 0, order, jnp.where(row == 1, slot, jnp.where(row == 2, c.astype(F32), 1.0))
        ).astype(BF16)
        tagged[dest] += lax.dot_general(tag, pick, NT, preferred_element_type=F32)

    @pl.when(step == pl.num_programs(0) - 1)
    def _():
        rows_ref[...] = held[...].astype(BF16)
        tags_ref[...] = tagged[...]
        flat = [jnp.sum(sums[i].T, axis=0, keepdims=True) for i in range(3)]
        mom_ref[...] = jnp.concatenate(flat + [jnp.zeros((5, coarse), F32)], axis=0)


def split3(v):
    a = v.astype(BF16).astype(F32)
    b = (v - a).astype(BF16).astype(F32)
    return [a, b, v - a - b]


def exchange_kernel(
    freq_count, drift_total, rows_ref, tags_ref, mom_ref, med_ref, mad_ref, snr_ref, keys_ref, excess_ref,
    other, rows_out, keys_out, rows_in, keys_in, mom_sem, row_send, row_recv, key_send, key_recv,
):
    me = lax.axis_index("freq")
    half = lax.axis_index("sub")
    coarse = mom_ref.shape[1]
    barrier = pltpu.get_barrier_semaphore()
    pl.semaphore_signal(barrier, inc=1, device_id={"sub": 1 - half}, device_id_type=MESH)
    for d in range(1, freq_count):
        pl.semaphore_signal(
            barrier, inc=1, device_id={"freq": lax.rem(me + d, freq_count)}, device_id_type=MESH
        )
    pl.semaphore_wait(barrier, freq_count)

    swap = pltpu.make_async_remote_copy(
        src_ref=mom_ref, dst_ref=other, send_sem=mom_sem.at[0], recv_sem=mom_sem.at[1],
        device_id={"sub": 1 - half}, device_id_type=MESH,
    )
    swap.start()
    swap.wait()
    moments = mom_ref[...] + other[...]
    floor_count = jnp.maximum(moments[0:1], 1.0)
    mad = mad_ref[...].astype(F32)
    mean_level = BIN_STEP * med_ref[...].astype(F32) + moments[1:2] / floor_count
    mad_sigma = MAD_SCALE * BIN_STEP * mad
    sigma = jnp.sqrt(0.5 * moments[2:3] / floor_count + 0.5 * mad_sigma * mad_sigma)
    table = jnp.concatenate(
        split3(mean_level) + split3(1.0 / sigma) + [jnp.zeros((2, coarse), F32)], axis=0
    ).astype(BF16)
    drift_dev = drift_total // lax.axis_size("sub")
    base = (half * (drift_dev * PER)).astype(F32)

    def prepare(o):
        tags = tags_ref[o]
        filled = tags[3:4] > 0.5
        hot = one((iota((coarse, CAP), 0).astype(F32) == tags[2:3]) & filled)
        vals = jnp.dot(table, hot, preferred_element_type=F32)
        level = vals[0:1] + vals[1:2] + vals[2:3]
        scale = vals[3:4] + vals[4:5] + vals[5:6]
        cols = jnp.concatenate([level, scale, jnp.zeros((6, CAP), F32)], axis=0).T
        rows_out[o] = ((rows_ref[o].astype(F32) - cols[:, 0:1]) * cols[:, 1:2]).astype(BF16)
        key = tags[1:2] * float(drift_total * PER) + base + tags[0:1]
        key = jnp.where(filled, key, -1.0).astype(jnp.int32)
        keys_out[o] = jnp.broadcast_to(key, (8, CAP))

    def send(d):
        to = lax.rem(me + d, freq_count)
        move = functools.partial(
            pltpu.make_async_remote_copy, device_id={"freq": to}, device_id_type=MESH
        )
        return (
            move(src_ref=rows_out.at[to], dst_ref=rows_in.at[me], send_sem=row_send.at[d], recv_sem=row_recv.at[d]),
            move(src_ref=keys_out.at[to], dst_ref=keys_in.at[me], send_sem=key_send.at[d], recv_sem=key_recv.at[d]),
        )

    for d in range(freq_count):
        prepare(lax.rem(me + d, freq_count))
    for d in range(1, freq_count):
        for copy in send(d):
            copy.start()
    rows_in[me] = rows_out[me]
    keys_in[me] = keys_out[me]
    for d in range(1, freq_count):
        for copy in send(d):
            copy.wait()

    begin = jnp.zeros((1, 1), F32)
    dst, key_row = [], []
    lanes = iota((1, CAP), 1).astype(F32)
    for f in range(freq_count):
        key = keys_in[f][0:1]
        live = key >= 0
        dst.append(jnp.where(live, begin + lanes, -1.0))
        key_row.append(key)
        begin = begin + jnp.sum(one(live, F32), axis=1, keepdims=True)
    dst = jnp.concatenate(dst, axis=1)
    key_row = jnp.concatenate(key_row, axis=1)
    width = freq_count * CAP
    digits = jnp.concatenate(
        [
            (key_row // 256).astype(F32),
            (key_row % 256).astype(F32),
            jnp.ones((1, width), F32),
            jnp.zeros((5, width), F32),
        ],
        axis=0,
    ).astype(BF16)
    spot = iota((CAP, width), 0).astype(F32).astype(BF16)
    arrived = rows_in[...].reshape(width, BLOCK)
    for k in range(freq_count):
        local = jnp.clip(dst - float(k * CAP), -1.0, float(CAP))
        line = jnp.broadcast_to(local, (16, width)).astype(BF16)
        pick = one(jnp.concatenate([line] * (CAP // 16), axis=0) == spot)
        out = jnp.dot(pick, arrived, preferred_element_type=F32)
        snr_ref[k * CAP : (k + 1) * CAP, :] = out.astype(BF16)
        got = lax.dot_general(digits, pick, NT, preferred_element_type=F32)
        key = jnp.where(got[2:3] > 0.5, got[0:1] * 256.0 + got[1:2], -1.0)
        keys_ref[:, k * CAP : (k + 1) * CAP] = key.astype(jnp.int32)
        over = jnp.maximum(out - THRESH, 0.0)
        excess_ref[:, k * CAP : (k + 1) * CAP] = jnp.sum(over.T, axis=0, keepdims=True)


def per_device(spectrum, hit_mask, owner_map, median_bin, mad_bin):
    drift_dev = spectrum.shape[0]
    coarse = owner_map.shape[0]
    freq_count = lax.axis_size("freq")
    drift_total = drift_dev * lax.axis_size("sub")
    width = freq_count * CAP
    chunk = 8
    smem = pl.BlockSpec(memory_space=pltpu.SMEM)
    vmem = pl.BlockSpec(memory_space=pltpu.VMEM)
    whole = lambda shape: pl.BlockSpec(shape, lambda i: (0,) * len(shape))
    rows, tags, moments = pl.pallas_call(
        local_kernel,
        grid=(coarse // chunk,),
        out_shape=(
            jax.ShapeDtypeStruct((freq_count, CAP, BLOCK), BF16),
            jax.ShapeDtypeStruct((freq_count, 8, CAP), F32),
            jax.ShapeDtypeStruct((8, coarse), F32),
        ),
        in_specs=[
            smem, smem, smem,
            whole((1, coarse)),
            whole((drift_dev, coarse * PER)),
            pl.BlockSpec((drift_dev, chunk * COARSE_WIDTH), lambda i: (0, i)),
        ],
        out_specs=(
            whole((freq_count, CAP, BLOCK)), whole((freq_count, 8, CAP)), whole((8, coarse))
        ),
        scratch_shapes=[
            pltpu.VMEM((coarse * PER, drift_dev), F32),
            pltpu.VMEM((coarse, PER * drift_dev), F32),
            pltpu.VMEM((freq_count, CAP, BLOCK), F32),
            pltpu.VMEM((freq_count, 8, CAP), F32),
            pltpu.VMEM((3, coarse, BLOCK), F32),
        ],
        compiler_params=pltpu.CompilerParams(dimension_semantics=("arbitrary",)),
        name="moments_and_pick",
    )(owner_map, median_bin, mad_bin, owner_map.reshape(1, coarse), hit_mask, spectrum)
    snr, keys, excess = pl.pallas_call(
        functools.partial(exchange_kernel, freq_count, drift_total),
        out_shape=(
            jax.ShapeDtypeStruct((width, BLOCK), BF16),
            jax.ShapeDtypeStruct((1, width), jnp.int32),
            jax.ShapeDtypeStruct((1, width), F32),
        ),
        in_specs=[vmem] * 5,
        out_specs=(vmem,) * 3,
        scratch_shapes=[
            pltpu.VMEM((8, coarse), F32),
            pltpu.VMEM((freq_count, CAP, BLOCK), BF16),
            pltpu.VMEM((freq_count, 8, CAP), jnp.int32),
            pltpu.VMEM((freq_count, CAP, BLOCK), BF16),
            pltpu.VMEM((freq_count, 8, CAP), jnp.int32),
            pltpu.SemaphoreType.DMA((2,)),
            pltpu.SemaphoreType.DMA((freq_count,)),
            pltpu.SemaphoreType.DMA((freq_count,)),
            pltpu.SemaphoreType.DMA((freq_count,)),
            pltpu.SemaphoreType.DMA((freq_count,)),
        ],
        compiler_params=pltpu.CompilerParams(collective_id=0, has_side_effects=True),
        name="exchange_and_list",
    )(rows, tags, moments, median_bin.reshape(1, coarse), mad_bin.reshape(1, coarse))
    return (
        snr.reshape(1, 1, width, BLOCK),
        keys.reshape(1, 1, width),
        excess.reshape(1, 1, width),
    )


def solution(mesh):
    placed = (
        P("sub", ("beam", "freq")),
        P("sub", ("beam", "freq")),
        P(("beam", "freq")),
        P(("beam", "freq")),
        P(("beam", "freq")),
    )
    return jax.shard_map(
        per_device,
        mesh=mesh,
        in_specs=placed,
        out_specs=(
            P("freq", "sub", "beam", None),
            P("freq", "sub", "beam"),
            P("freq", "sub", "beam"),
        ),
        check_vma=False,
    )
```

time: 82 us -> 37.6 us (0.46)
  local copies, waits for them, and re-layouts: 38.3 us -> 4.21 us
  Pallas kernels: 0 us -> 32.3 us
  other arithmetic: 22.3 us -> 0 us
  starting transfers between devices: 13.1 us -> 0 us
  waiting for transfers between devices: 2.74 us -> 0 us
  blocking collectives: 2.63 us -> 0 us
  matrix products: 1.37 us -> 0 us
    pallas_call x0 -> x2, Pallas kernels: none -> 32.3 us  [the longest x1 16.7 us: per_device(): pl.pallas_call(functools.partial(exchange_kernel, freq_count, drift_total...]
    gather x5 -> x0, local copies, waits for them, and re-layouts: 22.4 us -> none  [the longest x1 7.34 us: per_device(): blocks = spectrum.reshape(-1, BLOCK)[source_row]]
    reduce_sum x15 -> x0, other arithmetic: 16.1 us -> none  [the longest x2 10.8 us: per_device(): first = jnp.sum(kept, axis=(0, 2))]
    all_to_all x2 -> x0, starting transfers between devices: 13.1 us -> none  [the longest x1 7.16 us: per_device(): lax.all_to_all(slot_keys.reshape(freq_count, CAP), 'freq', split_axis=0,...]
    reshape x1 -> x0, local copies, waits for them, and re-layouts: 8.9 us -> none  [per_device(): blocks = spectrum.reshape(-1, BLOCK)[source_row]]
    select_n x10 -> x0, other arithmetic: 3.41 us -> none  [the longest x1 0.91 us: per_device(): jnp.where(live[:, None], hit_rows.reshape(-1, BLOCK)[take], jnp.zeros((1,...]
    reduce_sum x5 -> x0, local copies, waits for them, and re-layouts: 3.28 us -> none  [the longest x1 1.94 us: per_device(): second = jnp.sum(kept * kept, axis=(0, 2))]
    all_to_all x2 -> x0, waiting for transfers between devices: 2.74 us -> none  [the longest x1 2.74 us: per_device(): lax.all_to_all(payload.reshape(freq_count, CAP, BLOCK), 'freq', split_axi...]
  transfers between devices with their start and end apart: 2 -> 0, of which waited for: 1 -> 0; matrix products, arithmetic and copies ran while one was open for 29% -> 0% of each run, Pallas kernels for 0% -> 0%
where the time goes in v1:
time: 37.6 us; the launch traced here: 37.1 us
  Pallas kernels  32.3 us (86%)
  local copies, waits for them, and re-layouts  4.21 us (11%)
  between operations  0.64 us (2%)
    pallas_call x1, Pallas kernels, per_device(): pl.pallas_call(functools.partial(exchange_kernel, freq_count, drift_total...  16.7 us
    pallas_call x1, Pallas kernels, per_device(): pl.pallas_call(local_kernel, grid=(coarse // chunk,), out_shape=(jax.Shap...  15.6 us
    unnamed x3, local copies, waits for them, and re-layouts  4.21 us

profile of v1, /device:TPU:0, one launch (start us, length us, event | category | flops | bytes accessed | tf_op | source)
XLA Modules:
  0.0 37.1 jit_solution(14104410320930942740)
XLA Ops:
  0.6 15.6 %moments_and_pick.1 = (bf16[8,128,128]{2,1,0:T(8,128)(2,1)}, f32[8,8,128]{2,1,0:T(8,128)}, f32[8,128]{1,0:T(8,128)}) custom-call(s32[128]{0:T(128)} %om_s.1, s32[128]{0:T(128)} %med_s.1, s32[128]{0:T(128)} %mad_s.1, s32[1,128]{1,0:T(1,128)} %bitcast.9, s32[32,1024]{1,0:T(8,128)} %mask_ref.1, bf16[32,131072]{1,0:T(8,128)(2,1)} %spec_ref.1), custom_call_target="tpu_custom_call" | custom-call | tf_op jit(solution)/shard_map/moments_and_pick/pallas_call | solution.py:233
  16.2 16.7 %exchange_and_list.1 = (bf16[1024,128]{1,0:T(8,128)(2,1)}, s32[1,1024]{1,0:T(1,128)}, f32[1,1024]{1,0:T(1,128)}) custom-call(bf16[8,128,128]{2,1,0:T(8,128)(2,1)} %get-tuple-element.9.rows_ref, f32[8,8,128]{2,1,0:T(8,128)} %get-tuple-element.10.tags_ref, f32[8,128]{1,0:T(8,128)} %get-tuple-element.11.mom_ref, s32[1,128]{1,0:T(1,128)} %bitcast.10, ...), custom_call_target="tpu_custom_call" | custom-call | tf_op jit(solution)/shard_map/exchange_and_list/pallas_call | solution.py:260
  32.9 1.7 %copy.11 = bf16[1,1,1024,128]{3,2,1,0:T(8,128)(2,1)} copy(bf16[1,1,1024,128]{3,2,1,0:T(8,128)(2,1)} %bitcast.6) | data formatting | bytes 524288
  34.6 1.3 %copy.12 = s32[1,1,1024]{2,1,0:T(1,128)} copy(s32[1,1,1024]{2,1,0:T(1,128)} %bitcast.8) | data formatting | bytes 8192
  35.9 1.3 %copy.13 = f32[1,1,1024]{2,1,0:T(1,128)} copy(f32[1,1,1024]{2,1,0:T(1,128)} %bitcast.7) | data formatting | bytes 8192

commit v2 on v1

v2 whole, which is shorter than its diff:
```python
import functools

import jax
import jax.numpy as jnp
from jax import lax
from jax.experimental import pallas as pl
from jax.experimental.pallas import tpu as pltpu
from jax.sharding import PartitionSpec as P

COARSE_WIDTH = 1024
BLOCK = 128
CAP = 128
PER = COARSE_WIDTH // BLOCK

BIN_STEP = 0.0625
MAD_WIDTH = 5.0
MAD_SCALE = 1.4826
THRESH = 3.0

F32 = jnp.float32
BF16 = jnp.bfloat16
MESH = pl.DeviceIdType.MESH
NT = (((1,), (1,)), ((), ()))
UNROLL = 8
OUT_SPEC = pl.BlockSpec(memory_space=pl.ANY)


def iota(shape, dim):
    return lax.broadcasted_iota(jnp.int32, shape, dim)


def one(mask, dtype=BF16):
    return jnp.where(mask, jnp.ones((), dtype), jnp.zeros((), dtype))


def split3(v):
    a = v.astype(BF16).astype(F32)
    b = (v - a).astype(BF16).astype(F32)
    return [a, b, v - a - b]


def plan(om_ref, med_ref, mad_ref, mask_ref, turned, place, facts, inverse, quota):
    drifts = mask_ref.shape[0]
    coarse = place.shape[0]
    keys = PER * drifts
    wide = jnp.broadcast_to(om_ref[...], (coarse, coarse))
    down, across = iota((coarse, coarse), 0), iota((coarse, coarse), 1)
    tall = jnp.sum(jnp.where(down == across, wide, 0), axis=1, keepdims=True)
    rank_tall = jnp.sum(one(wide < tall, jnp.int32), axis=1, keepdims=True)
    rank_wide = jnp.sum(one(tall < wide, F32), axis=0, keepdims=True)
    found = jnp.sum(jnp.where(rank_tall == across, down, 0), axis=0, keepdims=True)
    inverse[...] = jnp.minimum(found, coarse - 1)
    sort = one(rank_wide == down.astype(F32))

    turned[...] = mask_ref[...].astype(F32).T
    marks = jnp.concatenate([turned[pl.ds(b, coarse, stride=PER), :] for b in range(PER)], axis=1)
    marks = jnp.dot(sort, marks.astype(BF16), preferred_element_type=F32)
    rank_a = iota((keys, keys), 0)
    rank_b = iota((keys, keys), 1)
    rank_a = (rank_a % drifts) * PER + rank_a // drifts
    rank_b = (rank_b % drifts) * PER + rank_b // drifts
    before = jnp.dot(marks.astype(BF16), one(rank_a < rank_b), preferred_element_type=F32)
    count = jnp.sum(marks, axis=1, keepdims=True)
    ahead = (down // quota == across // quota) & (across < down)
    offset = jnp.dot(
        one(ahead),
        jnp.broadcast_to(count, (coarse, keys)).astype(BF16),
        preferred_element_type=F32,
    )
    place[...] = jnp.where(marks > 0, offset + before, -1.0)

    med = med_ref[...]
    own = jnp.concatenate(
        [
            (med // 256).astype(F32),
            (med % 256).astype(F32),
            mad_ref[...].astype(F32),
            (om_ref[...] % coarse).astype(F32),
            jnp.zeros((4, coarse), F32),
        ],
        axis=0,
    ).astype(BF16)
    own = lax.dot_general(own, sort, NT, preferred_element_type=F32)
    facts[0:1, :] = BIN_STEP * (own[0:1] * 256.0 + own[1:2])
    facts[1:3, :] = own[2:4]


def send_kernel(
    freq_count, quota, om_ref, med_ref, mad_ref, med_s, mad_s, mask_ref, spec_ref,
    rows_in, tags_in, mom_in,
    buf, turned, place, facts, inverse, inverse_s, sums, rows_out, tags_out, mom_out,
    load_sem, inv_sem, own_sem, row_send, row_recv, tag_send, tag_recv, mom_send, mom_recv,
):
    me = lax.axis_index("freq")
    half = lax.axis_index("sub")
    drifts = mask_ref.shape[0]
    coarse = place.shape[0]
    keys = PER * drifts

    def load(c):
        at = pl.multiple_of(c * COARSE_WIDTH, COARSE_WIDTH)
        return pltpu.make_async_copy(
            spec_ref.at[:, pl.ds(at, COARSE_WIDTH)], buf.at[c], load_sem.at[c]
        )

    lax.fori_loop(0, coarse, lambda c, _: load(c).start(), None, unroll=4)

    others = [(d, s) for d in range(freq_count) for s in range(2) if d or s]

    def peer(d, s):
        return {"freq": lax.rem(me + d, freq_count), "sub": lax.rem(half + s, 2)}

    barrier = pltpu.get_barrier_semaphore()
    for d, s in others:
        pl.semaphore_signal(barrier, inc=1, device_id=peer(d, s), device_id_type=MESH)

    plan(om_ref, med_ref, mad_ref, mask_ref, turned, place, facts, inverse, quota)
    to_scalars = pltpu.make_async_copy(inverse, inverse_s, inv_sem.at[0])
    to_scalars.start()
    to_scalars.wait()
    lax.fori_loop(0, coarse, lambda c, _: load(c).wait(), None, unroll=4)
    pl.semaphore_wait(barrier, len(others))

    spot = iota((CAP, keys), 0).astype(F32).astype(BF16)
    lane = iota((8, keys), 1)
    row = iota((8, keys), 0)
    order = ((lane % drifts) * PER + lane // drifts).astype(F32)
    half_f = half.astype(F32)

    def channel(q, j):
        c = inverse_s[0, q]
        center = BIN_STEP * med_s[c].astype(F32)
        spread = MAD_WIDTH * BIN_STEP * mad_s[c].astype(F32)
        low, high = center - spread, center + spread
        total = [jnp.zeros((8, BLOCK), F32) for _ in range(3)]
        tiles = []
        for b in range(PER):
            tile = buf[c, :, b * BLOCK : (b + 1) * BLOCK]
            tiles.append(tile)
            x = tile.astype(F32)
            inside = (x >= low) & (x <= high)
            kept = jnp.where(inside, x - center, 0.0)
            for i, v in enumerate((one(inside, F32), kept, kept * kept)):
                for r in range(0, drifts, 8):
                    total[i] = total[i] + v[r : r + 8]
        for i in range(3):
            sums[i, pl.ds(q, 1), :] = jnp.sum(total[i], axis=0, keepdims=True)
        line = jnp.broadcast_to(place[pl.ds(q, 1), :], (16, keys)).astype(BF16)
        pick = one(jnp.concatenate([line] * (CAP // 16), axis=0) == spot)
        tag = jnp.where(
            row == 0,
            order,
            jnp.where(row == 1, j.astype(F32), jnp.where(row == 2, 1.0, jnp.where(row == 3, half_f, 0.0))),
        ).astype(BF16)
        return (
            jnp.dot(pick, jnp.concatenate(tiles, axis=0), preferred_element_type=F32),
            lax.dot_general(tag, pick, NT, preferred_element_type=F32),
        )

    def move(src, dst, send, recv, d, s):
        return pltpu.make_async_remote_copy(
            src_ref=src, dst_ref=dst, send_sem=send, recv_sem=recv,
            device_id=peer(d, s), device_id_type=MESH,
        )

    def hits(d):
        o = lax.rem(me + d, freq_count)
        return (
            move(rows_out.at[o], rows_in.at[me], row_send.at[d], row_recv.at[d], d, 0),
            move(tags_out.at[o], tags_in.at[me], tag_send.at[d], tag_recv.at[d], d, 0),
        )

    group = min(quota, UNROLL)

    def owner(step, _):
        d = lax.rem(step + 1, freq_count)
        o = lax.rem(me + d, freq_count)

        def some(p, carry):
            rows, tags = carry
            for u in range(group):
                j = p * group + u
                more = channel(o * quota + j, j)
                rows, tags = rows + more[0], tags + more[1]
            return rows, tags

        rows, tags = lax.fori_loop(
            0, quota // group, some, (jnp.zeros((CAP, BLOCK), F32), jnp.zeros((8, CAP), F32))
        )
        rows_out[o] = rows.astype(BF16)
        tags_out[o] = tags

        @pl.when(step < freq_count - 1)
        def _():
            for copy in hits(d):
                copy.start()

        return 0

    lax.fori_loop(0, freq_count, owner, 0)

    flat = [jnp.sum(sums[i].T, axis=0, keepdims=True) for i in range(3)]
    info = jnp.where(half == 0, facts[0:3, :], 0.0)
    tile = jnp.concatenate(flat + [info, jnp.zeros((2, coarse), F32)], axis=0)
    parts = jnp.concatenate(split3(tile), axis=0).astype(BF16)
    down, across = iota((coarse, coarse), 0), iota((coarse, coarse), 1)
    for o in range(freq_count):
        shift = one((down - o * quota == across - me * quota) & (across // quota == me))
        got = jnp.dot(parts, shift, preferred_element_type=F32)
        mom_out[o] = got[0:8] + got[8:16] + got[16:24]

    own = (
        pltpu.make_async_copy(rows_out.at[me], rows_in.at[me], own_sem.at[0]),
        pltpu.make_async_copy(tags_out.at[me], tags_in.at[me], own_sem.at[1]),
        pltpu.make_async_copy(mom_out.at[me], mom_in.at[me, half], own_sem.at[2]),
    )
    for copy in own:
        copy.start()
    moments = [
        move(
            mom_out.at[lax.rem(me + d, freq_count)], mom_in.at[me, half],
            mom_send.at[2 * d + s], mom_recv.at[2 * d + s], d, s,
        )
        for d, s in others
    ]
    for copy in moments:
        copy.start()
    for copy in own:
        copy.wait()
    for d in range(1, freq_count):
        for copy in hits(d):
            copy.wait()
    for copy in moments:
        copy.wait()


def list_kernel(freq_count, quota, drift_total, rows_ref, tags_ref, mom_ref, snr_ref, keys_ref, excess_ref):
    coarse = mom_ref.shape[3]
    width = freq_count * CAP
    table = jnp.zeros((8, coarse), F32)
    for f in range(freq_count):
        table = table + (mom_ref[f, 0] + mom_ref[f, 1])
    floor_count = jnp.maximum(table[0:1], 1.0)
    mean_level = table[3:4] + table[1:2] / floor_count
    mad_sigma = MAD_SCALE * BIN_STEP * table[4:5]
    sigma = jnp.sqrt(0.5 * table[2:3] / floor_count + 0.5 * mad_sigma * mad_sigma)
    lookup = jnp.concatenate(
        split3(mean_level) + split3(1.0 / sigma) + [table[5:6], jnp.zeros((1, coarse), F32)], axis=0
    ).astype(BF16)

    begin = jnp.zeros((1, 1), F32)
    dst, digits = [], []
    lanes = iota((1, CAP), 1).astype(F32)
    row = iota((8, CAP), 0)
    for f in range(freq_count):
        tags = tags_ref[f]
        live = tags[2:3] > 0.5
        dst.append(jnp.where(live, begin + lanes, -1.0))
        digits.append(tags + jnp.where(row == 1, float(f * quota), 0.0))
        begin = begin + jnp.sum(one(live, F32), axis=1, keepdims=True)
    dst = jnp.concatenate(dst, axis=1)
    digits = jnp.concatenate(digits, axis=1).astype(BF16)
    spot = iota((CAP, width), 0).astype(F32).astype(BF16)
    arrived = rows_ref[...].reshape(width, BLOCK)
    index = iota((coarse, CAP), 0).astype(F32)

    def block(k, at):
        local = jnp.clip(dst - k * float(CAP), -1.0, float(CAP))
        line = jnp.broadcast_to(local, (16, width)).astype(BF16)
        pick = one(jnp.concatenate([line] * (CAP // 16), axis=0) == spot)
        raw = jnp.dot(pick, arrived, preferred_element_type=F32)
        got = lax.dot_general(digits, pick, NT, preferred_element_type=F32)
        filled = got[2:3] > 0.5
        hot = one((index == got[1:2]) & filled)
        vals = jnp.dot(lookup, hot, preferred_element_type=F32)
        level = vals[0:1] + vals[1:2] + vals[2:3]
        scale = vals[3:4] + vals[4:5] + vals[5:6]
        cols = jnp.concatenate([level, scale, jnp.zeros((6, CAP), F32)], axis=0).T
        snr = ((raw - cols[:, 0:1]) * cols[:, 1:2]).astype(BF16)
        snr_ref[pl.ds(at, CAP), :] = snr
        key = vals[6:7] * float(drift_total * PER) + got[3:4] * float(drift_total // 2 * PER) + got[0:1]
        keys_ref[:, pl.ds(at, CAP)] = jnp.where(filled, key, -1.0).astype(jnp.int32)
        over = jnp.maximum(snr.astype(F32) - THRESH, 0.0)
        excess_ref[:, pl.ds(at, CAP)] = jnp.sum(over.T, axis=0, keepdims=True)

    if freq_count <= 8:
        for k in range(freq_count):
            block(float(k), k * CAP)
    else:

        @pl.loop(0, freq_count)
        def _(k):
            block(k.astype(F32), pl.multiple_of(k * CAP, CAP))


def per_device(spectrum, hit_mask, owner_map, median_bin, mad_bin):
    drift_dev = spectrum.shape[0]
    coarse = owner_map.shape[0]
    freq_count = lax.axis_size("freq")
    drift_total = drift_dev * lax.axis_size("sub")
    width = freq_count * CAP
    quota = coarse // freq_count
    smem = pl.BlockSpec(memory_space=pltpu.SMEM)
    vmem = pl.BlockSpec(memory_space=pltpu.VMEM)
    anyw = pl.BlockSpec(memory_space=pl.ANY)
    dma = pltpu.SemaphoreType.DMA
    rows, tags, moments = pl.pallas_call(
        functools.partial(send_kernel, freq_count, quota),
        out_shape=(
            jax.ShapeDtypeStruct((freq_count, CAP, BLOCK), BF16),
            jax.ShapeDtypeStruct((freq_count, 8, CAP), F32),
            jax.ShapeDtypeStruct((freq_count, 2, 8, coarse), F32),
        ),
        in_specs=[vmem, vmem, vmem, smem, smem, vmem, anyw],
        out_specs=(OUT_SPEC,) * 3,
        scratch_shapes=[
            pltpu.VMEM((coarse, drift_dev, COARSE_WIDTH), BF16),
            pltpu.VMEM((coarse * PER, drift_dev), F32),
            pltpu.VMEM((coarse, PER * drift_dev), F32),
            pltpu.VMEM((8, coarse), F32),
            pltpu.VMEM((1, coarse), jnp.int32),
            pltpu.SMEM((1, coarse), jnp.int32),
            pltpu.VMEM((3, coarse, BLOCK), F32),
            pltpu.VMEM((freq_count, CAP, BLOCK), BF16),
            pltpu.VMEM((freq_count, 8, CAP), F32),
            pltpu.VMEM((freq_count, 8, coarse), F32),
            dma((coarse,)),
            dma((1,)),
            dma((3,)),
            dma((freq_count,)),
            dma((freq_count,)),
            dma((freq_count,)),
            dma((freq_count,)),
            dma((2 * freq_count,)),
            dma((2 * freq_count,)),
        ],
        compiler_params=pltpu.CompilerParams(collective_id=0, has_side_effects=True),
        name="moments_pick_send",
    )(
        owner_map.reshape(1, coarse),
        median_bin.reshape(1, coarse),
        mad_bin.reshape(1, coarse),
        median_bin,
        mad_bin,
        hit_mask,
        spectrum,
    )
    snr, keys, excess = pl.pallas_call(
        functools.partial(list_kernel, freq_count, quota, drift_total),
        out_shape=(
            jax.ShapeDtypeStruct((width, BLOCK), BF16),
            jax.ShapeDtypeStruct((1, width), jnp.int32),
            jax.ShapeDtypeStruct((1, width), F32),
        ),
        in_specs=[vmem] * 3,
        out_specs=(vmem,) * 3,
        name="normalize_and_list",
    )(rows, tags, moments)
    return (
        snr.reshape(1, 1, width, BLOCK),
        keys.reshape(1, 1, width),
        excess.reshape(1, 1, width),
    )


def solution(mesh):
    placed = (
        P("sub", ("beam", "freq")),
        P("sub", ("beam", "freq")),
        P(("beam", "freq")),
        P(("beam", "freq")),
        P(("beam", "freq")),
    )
    return jax.shard_map(
        per_device,
        mesh=mesh,
        in_specs=placed,
        out_specs=(
            P("freq", "sub", "beam", None),
            P("freq", "sub", "beam"),
            P("freq", "sub", "beam"),
        ),
        check_vma=False,
    )
```

time: 37.6 us -> 30.3 us (0.81)
  local copies, waits for them, and re-layouts: 4.21 us -> 0 us
  Pallas kernels: 32.3 us -> 29.5 us
    unnamed x3 -> x0, local copies, waits for them, and re-layouts: 4.21 us -> none
    pallas_call x2, Pallas kernels: 32.3 us -> 29.5 us  [the longest x1 24.3 us: per_device(): pl.pallas_call(functools.partial(send_kernel, freq_count, quota), out_sha...]
where the time goes in v2:
time: 30.3 us; the launch traced here: 30.1 us
  Pallas kernels  29.5 us (97%)
  between operations  0.64 us (2%)
    pallas_call x1, Pallas kernels, per_device(): pl.pallas_call(functools.partial(send_kernel, freq_count, quota), out_sha...  24.3 us
    pallas_call x1, Pallas kernels, per_device(): pl.pallas_call(functools.partial(list_kernel, freq_count, quota, drift_to...  5.12 us

profile of v2, /device:TPU:0, one launch (start us, length us, event | category | flops | bytes accessed | tf_op | source)
XLA Modules:
  0.0 30.1 jit_solution(2245044935978186361)
XLA Ops:
  0.6 24.3 %moments_pick_send.1 = (bf16[8,128,128]{2,1,0:T(8,128)(2,1)}, f32[8,8,128]{2,1,0:T(8,128)}, f32[8,2,8,128]{3,2,1,0:T(8,128)}) custom-call(s32[1,128]{1,0:T(1,128)} %bitcast.8, s32[1,128]{1,0:T(1,128)} %bitcast.6, s32[1,128]{1,0:T(1,128)} %bitcast.7, s32[128]{0:T(128)} %med_s.1, s32[128]{0:T(128)} %mad_s.1, s32[32,1024]{1,0:T(8,128)} %mask_ref.1, ...), custom_call_target="tpu_custom_call" | custom-call | tf_op jit(solution)/shard_map/moments_pick_send/pallas_call | solution.py:307
  25.0 5.1 %normalize_and_list.1 = (bf16[1024,128]{1,0:T(8,128)(2,1)}, s32[1,1024]{1,0:T(1,128)}, f32[1,1024]{1,0:T(1,128)}) custom-call(bf16[8,128,128]{2,1,0:T(8,128)(2,1)} %get-tuple-element.9.rows_ref, f32[8,8,128]{2,1,0:T(8,128)} %get-tuple-element.10.tags_ref, f32[8,2,8,128]{3,2,1,0:T(8,128)} %get-tuple-element.11.mom_ref), custom_call_target="tpu_custom_call" | custom-call | tf_op jit(solution)/shard_map/normalize_and_list/pallas_call | solution.py:348

commit v3 on v2

--- a/solution.py
+++ b/solution.py
@@ -21,7 +21,7 @@
 BF16 = jnp.bfloat16
 MESH = pl.DeviceIdType.MESH
 NT = (((1,), (1,)), ((), ()))
-UNROLL = 8
+UNROLL = 16
 OUT_SPEC = pl.BlockSpec(memory_space=pl.ANY)
 
 
@@ -39,7 +39,7 @@
     return [a, b, v - a - b]
 
 
-def plan(om_ref, med_ref, mad_ref, mask_ref, turned, place, facts, inverse, quota):
+def plan(om_ref, med_ref, mad_ref, mask_ref, turned, place, mom_out, inverse, freq_count, quota, me, half):
     drifts = mask_ref.shape[0]
     coarse = place.shape[0]
     keys = PER * drifts
@@ -81,14 +81,18 @@
         axis=0,
     ).astype(BF16)
     own = lax.dot_general(own, sort, NT, preferred_element_type=F32)
-    facts[0:1, :] = BIN_STEP * (own[0:1] * 256.0 + own[1:2])
-    facts[1:3, :] = own[2:4]
+    for o in range(freq_count):
+        shift = one((down - o * quota == across - me * quota) & (across // quota == me))
+        got = jnp.dot(own.astype(BF16), shift, preferred_element_type=F32)
+        center = BIN_STEP * (got[0:1] * 256.0 + got[1:2])
+        info = jnp.concatenate([jnp.zeros((3, coarse), F32), center, got[2:4], jnp.zeros((2, coarse), F32)], axis=0)
+        mom_out[o] = jnp.where(half == 0, info, 0.0)
 
 
 def send_kernel(
     freq_count, quota, om_ref, med_ref, mad_ref, med_s, mad_s, mask_ref, spec_ref,
     rows_in, tags_in, mom_in,
-    buf, turned, place, facts, inverse, inverse_s, sums, rows_out, tags_out, mom_out,
+    buf, turned, place, inverse, inverse_s, sums, rows_out, tags_out, mom_out,
     load_sem, inv_sem, own_sem, row_send, row_recv, tag_send, tag_recv, mom_send, mom_recv,
 ):
     me = lax.axis_index("freq")
@@ -100,7 +104,7 @@
     def load(c):
         at = pl.multiple_of(c * COARSE_WIDTH, COARSE_WIDTH)
         return pltpu.make_async_copy(
-            spec_ref.at[:, pl.ds(at, COARSE_WIDTH)], buf.at[c], load_sem.at[c]
+            spec_ref.at[:, pl.ds(at, COARSE_WIDTH)], buf.at[c], load_sem.at[0]
         )
 
     lax.fori_loop(0, coarse, lambda c, _: load(c).start(), None, unroll=4)
@@ -114,11 +118,11 @@
     for d, s in others:
         pl.semaphore_signal(barrier, inc=1, device_id=peer(d, s), device_id_type=MESH)
 
-    plan(om_ref, med_ref, mad_ref, mask_ref, turned, place, facts, inverse, quota)
+    plan(om_ref, med_ref, mad_ref, mask_ref, turned, place, mom_out, inverse, freq_count, quota, me, half)
     to_scalars = pltpu.make_async_copy(inverse, inverse_s, inv_sem.at[0])
     to_scalars.start()
     to_scalars.wait()
-    lax.fori_loop(0, coarse, lambda c, _: load(c).wait(), None, unroll=4)
+    pltpu.make_async_copy(buf, buf, load_sem.at[0]).wait()
     pl.semaphore_wait(barrier, len(others))
 
     spot = iota((CAP, keys), 0).astype(F32).astype(BF16)
@@ -170,6 +174,12 @@
             move(tags_out.at[o], tags_in.at[me], tag_send.at[d], tag_recv.at[d], d, 0),
         )
 
+    def level(d, s):
+        return move(
+            mom_out.at[lax.rem(me + d, freq_count)], mom_in.at[me, half],
+            mom_send.at[2 * d + s], mom_recv.at[2 * d + s], d, s,
+        )
+
     group = min(quota, UNROLL)
 
     def owner(step, _):
@@ -189,49 +199,38 @@
         )
         rows_out[o] = rows.astype(BF16)
         tags_out[o] = tags
+        sub = iota((quota, coarse), 0)
+        mine = iota((quota, coarse), 1) == me * quota + sub
+        flat = []
+        for i in range(3):
+            each = jnp.sum(sums[i, pl.ds(o * quota, quota), :], axis=1, keepdims=True)
+            flat.append(jnp.sum(jnp.where(mine, each, 0.0), axis=0, keepdims=True))
+        mom_out[o] += jnp.concatenate(flat + [jnp.zeros((5, coarse), F32)], axis=0)
 
         @pl.when(step < freq_count - 1)
         def _():
-            for copy in hits(d):
+            for copy in hits(d) + (level(d, 0), level(d, 1)):
                 copy.start()
 
         return 0
 
     lax.fori_loop(0, freq_count, owner, 0)
 
-    flat = [jnp.sum(sums[i].T, axis=0, keepdims=True) for i in range(3)]
-    info = jnp.where(half == 0, facts[0:3, :], 0.0)
-    tile = jnp.concatenate(flat + [info, jnp.zeros((2, coarse), F32)], axis=0)
-    parts = jnp.concatenate(split3(tile), axis=0).astype(BF16)
-    down, across = iota((coarse, coarse), 0), iota((coarse, coarse), 1)
-    for o in range(freq_count):
-        shift = one((down - o * quota == across - me * quota) & (across // quota == me))
-        got = jnp.dot(parts, shift, preferred_element_type=F32)
-        mom_out[o] = got[0:8] + got[8:16] + got[16:24]
-
+    level(0, 1).start()
     own = (
         pltpu.make_async_copy(rows_out.at[me], rows_in.at[me], own_sem.at[0]),
         pltpu.make_async_copy(tags_out.at[me], tags_in.at[me], own_sem.at[1]),
         pltpu.make_async_copy(mom_out.at[me], mom_in.at[me, half], own_sem.at[2]),
     )
     for copy in own:
-        copy.start()
-    moments = [
-        move(
-            mom_out.at[lax.rem(me + d, freq_count)], mom_in.at[me, half],
-            mom_send.at[2 * d + s], mom_recv.at[2 * d + s], d, s,
-        )
-        for d, s in others
-    ]
-    for copy in moments:
         copy.start()
     for copy in own:
         copy.wait()
     for d in range(1, freq_count):
         for copy in hits(d):
             copy.wait()
-    for copy in moments:
-        copy.wait()
+    for d, s in others:
+        level(d, s).wait()
 
 
 def list_kernel(freq_count, quota, drift_total, rows_ref, tags_ref, mom_ref, snr_ref, keys_ref, excess_ref):
@@ -317,14 +316,13 @@
             pltpu.VMEM((coarse, drift_dev, COARSE_WIDTH), BF16),
             pltpu.VMEM((coarse * PER, drift_dev), F32),
             pltpu.VMEM((coarse, PER * drift_dev), F32),
-            pltpu.VMEM((8, coarse), F32),
             pltpu.VMEM((1, coarse), jnp.int32),
             pltpu.SMEM((1, coarse), jnp.int32),
             pltpu.VMEM((3, coarse, BLOCK), F32),
             pltpu.VMEM((freq_count, CAP, BLOCK), BF16),
             pltpu.VMEM((freq_count, 8, CAP), F32),
             pltpu.VMEM((freq_count, 8, coarse), F32),
-            dma((coarse,)),
+            dma((1,)),
             dma((1,)),
             dma((3,)),
             dma((freq_count,)),

time: 30.3 us -> 24.8 us (0.82)
  Pallas kernels: 29.5 us -> 23.9 us
    pallas_call x1, Pallas kernels: 24.3 us -> 18.8 us  [per_device(): pl.pallas_call(functools.partial(send_kernel, freq_count, quota), out_sha...]
where the time goes in v3:
time: 24.8 us; the launch traced here: 24.6 us
  Pallas kernels  23.9 us (96%)
  between operations  0.64 us (3%)
    pallas_call x1, Pallas kernels, per_device(): pl.pallas_call(functools.partial(send_kernel, freq_count, quota), out_sha...  18.8 us
    pallas_call x1, Pallas kernels, per_device(): pl.pallas_call(functools.partial(list_kernel, freq_count, quota, drift_to...  5.12 us

profile of v3, /device:TPU:0, one launch (start us, length us, event | category | flops | bytes accessed | tf_op | source)
XLA Modules:
  0.0 24.6 jit_solution(14396490254845098398)
XLA Ops:
  0.6 18.8 %moments_pick_send.1 = (bf16[8,128,128]{2,1,0:T(8,128)(2,1)}, f32[8,8,128]{2,1,0:T(8,128)}, f32[8,2,8,128]{3,2,1,0:T(8,128)}) custom-call(s32[1,128]{1,0:T(1,128)} %bitcast.8, s32[1,128]{1,0:T(1,128)} %bitcast.6, s32[1,128]{1,0:T(1,128)} %bitcast.7, s32[128]{0:T(128)} %med_s.1, s32[128]{0:T(128)} %mad_s.1, s32[32,1024]{1,0:T(8,128)} %mask_ref.1, ...), custom_call_target="tpu_custom_call" | custom-call | tf_op jit(solution)/shard_map/moments_pick_send/pallas_call | solution.py:306
  19.4 5.1 %normalize_and_list.1 = (bf16[1024,128]{1,0:T(8,128)(2,1)}, s32[1,1024]{1,0:T(1,128)}, f32[1,1024]{1,0:T(1,128)}) custom-call(bf16[8,128,128]{2,1,0:T(8,128)(2,1)} %get-tuple-element.9.rows_ref, f32[8,8,128]{2,1,0:T(8,128)} %get-tuple-element.10.tags_ref, f32[8,2,8,128]{3,2,1,0:T(8,128)} %get-tuple-element.11.mom_ref), custom_call_target="tpu_custom_call" | custom-call | tf_op jit(solution)/shard_map/normalize_and_list/pallas_call | solution.py:346
